TPU v7x, 128 devices: a whole 4x4x4 slice. The times are simulated.
128 devices in a mesh: dp: 1, cpo: 2 (over core), cpi: 64 (over z, y, x).
Axes of the slice: x: 4, y: 4, z: 4, core: 2. Of those that a mesh axis runs over, the one named last changes fastest.
Arguments:
- hidden: bfloat16 [32768, 4608], P(('dp', 'cpo', 'cpi'))
- w_q: bfloat16 [4608, 32, 128], replicated
- w_k: bfloat16 [4608, 16, 128], replicated
- w_v: bfloat16 [4608, 16, 128], replicated
- w_o: bfloat16 [32, 128, 4608], replicated
Outputs:
- output: bfloat16 [32768, 4608], P(('dp', 'cpo', 'cpi'))
All inputs are finite; a program needn't handle non-finite values.
Results may differ from a plain program's by a relative error of at most 0.00592278.
Values are sent between devices in bfloat16 or wider.
A program may use at most 1 GiB of HBM per device.

v0:
```python
import functools
import math

import jax
import jax.numpy as jnp
from jax import lax
from jax.experimental import pallas as pl
from jax.experimental.pallas import tpu as pltpu
from jax.sharding import PartitionSpec as P

ROPE_BASE = 10000.0
GROUP = 16
TOK = 256
HD = 128
BACK = 8
MESH = pl.DeviceIdType.MESH


def head_of(member):
    y = member // 4
    x = member % 4
    d = (x + 4 - y) % 4
    return 8 * (d % 2) + 4 * (d // 2) + y


def member_of(head):
    c = head // 8
    b = (head // 4) % 2
    y = head % 4
    return 4 * y + (y + c + 2 * b) % 4


def body(x_hbm, wq_hbm, wk_hbm, wv_hbm, wo_hbm, cos_hbm, sin_hbm, y_hbm,
         x_v, cos_v, sin_v, w0, w1, kv_out, q_out, kv_in, q_in, s_buf, o_out, o_in, wo_buf, y_acc, y_bf,
         in_sem, w_sem, wo_sem, y_sem, kv_ss, kv_rs, h_ss, h_rs, q_ss, q_rs, o_ss, o_rs):
    core = lax.axis_index('cpo')
    chip = lax.axis_index('cpi')
    z = chip // GROUP
    me = chip % GROUP
    base = z * GROUP
    my_head = head_of(me)
    d_model = x_v.shape[1]

    wk_first = pltpu.make_async_copy(wk_hbm.at[:, pl.ds(0, 8), :], w0, w_sem.at[0])
    wv_first = pltpu.make_async_copy(wv_hbm.at[:, pl.ds(0, 8), :], w1, w_sem.at[1])
    x_copy = pltpu.make_async_copy(x_hbm, x_v, in_sem.at[0])
    cos_copy = pltpu.make_async_copy(cos_hbm, cos_v, in_sem.at[1])
    sin_copy = pltpu.make_async_copy(sin_hbm, sin_v, in_sem.at[2])
    x_copy.start()
    cos_copy.start()
    sin_copy.start()
    wk_first.start()
    wv_first.start()

    next_core = jnp.where(z == 3, 1 - core, core)
    next_chip = ((z + 1) % 4) * GROUP + me
    prev_core = jnp.where(z == 0, 1 - core, core)
    prev_chip = ((z + 3) % 4) * GROUP + me

    barrier = pltpu.get_barrier_semaphore()
    for step in range(1, GROUP):
        pl.semaphore_signal(barrier, inc=1, device_id={'cpi': base + (me + step) % GROUP}, device_id_type=MESH)
    pl.semaphore_signal(barrier, inc=1, device_id={'cpo': next_core, 'cpi': next_chip}, device_id_type=MESH)
    pl.semaphore_signal(barrier, inc=1, device_id={'cpo': prev_core, 'cpi': prev_chip}, device_id_type=MESH)
    pl.semaphore_wait(barrier, GROUP + 1)

    x_copy.wait()
    cos_copy.wait()
    sin_copy.wait()

    def project(w_ref):
        w = w_ref[...].reshape(d_model, 8 * HD)
        return jnp.dot(x_v[...], w, preferred_element_type=jnp.float32)

    def rope(u):
        return u * cos_v[...] + pltpu.roll(u, HD // 2, 1) * sin_v[...]

    def kv_send(head):
        return pltpu.make_async_remote_copy(
            src_ref=kv_out.at[head], dst_ref=kv_in.at[BACK + me], send_sem=kv_ss.at[head], recv_sem=kv_rs.at[me],
            device_id={'cpi': base + member_of(head)}, device_id_type=MESH)

    def q_send(head):
        return pltpu.make_async_remote_copy(
            src_ref=q_out.at[head], dst_ref=q_in.at[me], send_sem=q_ss.at[head], recv_sem=q_rs.at[me],
            device_id={'cpi': base + member_of(head)}, device_id_type=MESH)

    def kv_recv(src):
        return pltpu.make_async_remote_copy(
            src_ref=kv_in.at[BACK + src], dst_ref=kv_in.at[BACK + src], send_sem=kv_ss.at[0], recv_sem=kv_rs.at[src],
            device_id={'cpi': base + src}, device_id_type=MESH)

    def q_recv(src):
        return pltpu.make_async_remote_copy(
            src_ref=q_in.at[src], dst_ref=q_in.at[src], send_sem=q_ss.at[0], recv_sem=q_rs.at[src],
            device_id={'cpi': base + src}, device_id_type=MESH)

    def halo(block):
        return pltpu.make_async_remote_copy(
            src_ref=kv_in.at[GROUP + block], dst_ref=kv_in.at[block], send_sem=h_ss.at[block], recv_sem=h_rs.at[block],
            device_id={'cpo': next_core, 'cpi': next_chip}, device_id_type=MESH)

    def o_send(block):
        return pltpu.make_async_remote_copy(
            src_ref=o_out.at[block], dst_ref=o_in.at[my_head], send_sem=o_ss.at[block], recv_sem=o_rs.at[my_head],
            device_id={'cpi': base + block}, device_id_type=MESH)

    def o_recv(head):
        return pltpu.make_async_remote_copy(
            src_ref=o_in.at[head], dst_ref=o_in.at[head], send_sem=o_ss.at[0], recv_sem=o_rs.at[head],
            device_id={'cpi': base + member_of(head)}, device_id_type=MESH)

    my_y = me // 4

    def kv_chunk(c, carry):
        pltpu.make_async_copy(wk_hbm.at[:, pl.ds(0, 8), :], w0, w_sem.at[0]).wait()
        k_all = project(w0)
        for i in range(8):
            kv_out[8 * c + i, 0:TOK, :] = rope(k_all[:, HD * i:HD * i + HD]).astype(jnp.bfloat16)

        @pl.when(c == 0)
        def _():
            pltpu.make_async_copy(wk_hbm.at[:, pl.ds(8, 8), :], w0, w_sem.at[0]).start()

        @pl.when(c == 1)
        def _():
            pltpu.make_async_copy(wq_hbm.at[:, pl.ds(0, 8), :], w0, w_sem.at[0]).start()

        pltpu.make_async_copy(wv_hbm.at[:, pl.ds(0, 8), :], w1, w_sem.at[1]).wait()
        v_all = project(w1)
        for i in range(8):
            v_bf = v_all[:, HD * i:HD * i + HD].astype(jnp.bfloat16)
            kv_out[8 * c + i, TOK:TOK + HD, :] = v_bf[0:HD].T
            kv_out[8 * c + i, TOK + HD:TOK + 2 * HD, :] = v_bf[HD:TOK].T

        @pl.when(c == 0)
        def _():
            pltpu.make_async_copy(wv_hbm.at[:, pl.ds(8, 8), :], w1, w_sem.at[1]).start()

        @pl.when(c == 1)
        def _():
            pltpu.make_async_copy(wq_hbm.at[:, pl.ds(8, 8), :], w1, w_sem.at[1]).start()

        for step in range(4):
            for b in range(2):
                head = 8 * c + 4 * b + (my_y + step) % 4

                @pl.when(head != my_head)
                def _():
                    kv_send(head).start()
        return carry

    lax.fori_loop(0, 2, kv_chunk, 0)

    def q_half(slot_ref, j):
        q_all = project(slot_ref)
        for i in range(4):
            for g in range(2):
                lo = HD * (2 * i + g)
                q_out[4 * j + i, TOK * g:TOK * g + TOK, :] = rope(q_all[:, lo:lo + HD]).astype(jnp.bfloat16)

    def q_sends(j):
        for step in range(4):
            head = 4 * j + (my_y + step) % 4

            @pl.when(head != my_head)
            def _():
                q_send(head).start()

    def q_chunk(c, carry):
        pltpu.make_async_copy(wq_hbm.at[:, pl.ds(0, 8), :], w0, w_sem.at[0]).wait()
        q_half(w0, 2 * c)

        @pl.when(c == 0)
        def _():
            pltpu.make_async_copy(wq_hbm.at[:, pl.ds(16, 8), :], w0, w_sem.at[0]).start()

        q_sends(2 * c)
        pltpu.make_async_copy(wq_hbm.at[:, pl.ds(0, 8), :], w1, w_sem.at[1]).wait()
        q_half(w1, 2 * c + 1)

        @pl.when(c == 0)
        def _():
            pltpu.make_async_copy(wq_hbm.at[:, pl.ds(24, 8), :], w1, w_sem.at[1]).start()

        q_sends(2 * c + 1)
        return carry

    lax.fori_loop(0, 2, q_chunk, 0)

    n_wo = wo_buf.shape[0]

    def wo_copy(g):
        return pltpu.make_async_copy(wo_hbm.at[pl.ds(4 * g, 4)], wo_buf.at[g % n_wo], wo_sem.at[g % n_wo])

    for g in range(n_wo):
        wo_copy(g).start()

    kv_in[BACK + me] = kv_out[my_head]
    q_in[me] = q_out[my_head]

    def kv_low(step, carry):
        src = step

        @pl.when(src != me)
        def _():
            kv_recv(src).wait_recv()

        @pl.when(src >= BACK)
        def _():
            halo(src - BACK).start()
        return carry

    lax.fori_loop(0, GROUP, kv_low, 0)

    scale = HD ** -0.5 * math.log2(math.e)
    rows_k = lax.broadcasted_iota(jnp.int32, (TOK, 2 * TOK), 0)
    rows_q = lax.broadcasted_iota(jnp.int32, (TOK, 2 * TOK), 1) % TOK
    causal = rows_k <= rows_q
    is_first = (z == 0) & (core == 0)
    neg = jnp.float32(-jnp.inf)

    def scores(block, q):
        return lax.dot_general(kv_in[block, 0:TOK, :], q, (((1,), (1,)), ((), ())), preferred_element_type=jnp.float32)

    def v_of(block):
        return jnp.concatenate([kv_in[block, TOK:TOK + HD, :], kv_in[block, TOK + HD:TOK + 2 * HD, :]], axis=1)

    def attend(i):
        q = q_in[i]
        bias = [jnp.where(is_first & (i + j < BACK), neg, jnp.float32(0.0)) for j in range(BACK)]
        merged = jnp.where(causal, scores(i + BACK, q), scores(i, q) + bias[0])
        s_buf[0] = merged
        top = jnp.max(merged, axis=0, keepdims=True)
        for j in range(1, BACK):
            s = scores(i + j, q)
            s_buf[j] = s
            top = jnp.maximum(top, jnp.max(s, axis=0, keepdims=True) + bias[j])
        top = top * scale
        p = jnp.exp2(s_buf[0] * scale - top)
        total = jnp.sum(p, axis=0, keepdims=True)
        zero = jnp.zeros_like(p)
        acc = jnp.dot(v_of(i + BACK), jnp.where(causal, p, zero).astype(jnp.bfloat16), preferred_element_type=jnp.float32)
        acc += jnp.dot(v_of(i), jnp.where(causal, zero, p).astype(jnp.bfloat16), preferred_element_type=jnp.float32)
        for j in range(1, BACK):
            p = jnp.exp2(s_buf[j] * scale - (top - bias[j]))
            total += jnp.sum(p, axis=0, keepdims=True)
            acc += jnp.dot(v_of(i + j), p.astype(jnp.bfloat16), preferred_element_type=jnp.float32)
        o = (acc / total).T
        o_out[i, :, 0:HD] = o[0:TOK].astype(jnp.bfloat16)
        o_out[i, :, HD:2 * HD] = o[TOK:2 * TOK].astype(jnp.bfloat16)

    def attend_step(t, carry):
        i = jnp.where(t < 8, 8, 0) + (me + t) % 8

        @pl.when(i != me)
        def _():
            q_recv(i).wait_recv()

        @pl.when(t == 8)
        def _():
            for b in range(BACK):
                halo(b).wait_recv()

        attend(i)

        @pl.when(i != me)
        def _():
            o_send(i).start()
        return carry

    lax.fori_loop(0, GROUP, attend_step, 0)

    o_in[my_head] = o_out[me]

    def out_step(g, carry):
        wo_copy(g).wait()
        for k in range(2):
            @pl.when(2 * g + k != my_head)
            def _():
                o_recv(2 * g + k).wait_recv()
        o = jnp.concatenate([o_in[2 * g], o_in[2 * g + 1]], axis=1)
        w = wo_buf[g % n_wo].reshape(4 * HD, d_model)
        part = jnp.dot(o, w, preferred_element_type=jnp.float32)

        @pl.when(g == 0)
        def _():
            y_acc[...] = part

        @pl.when(g > 0)
        def _():
            y_acc[...] += part

        @pl.when(g + n_wo < 8)
        def _():
            wo_copy(g + n_wo).start()
        return carry

    lax.fori_loop(0, 8, out_step, 0)
    y_bf[...] = y_acc[...].astype(jnp.bfloat16)
    y_copy = pltpu.make_async_copy(y_bf, y_hbm, y_sem)
    y_copy.start()

    for b in range(BACK):
        halo(b).wait_send()

    def drain(h, carry):
        @pl.when(h != my_head)
        def _():
            kv_send(h).wait_send()
            q_send(h).wait_send()

        @pl.when(h != me)
        def _():
            o_send(h).wait_send()
        return carry

    lax.fori_loop(0, GROUP, drain, 0)
    y_copy.wait()


def solution(mesh):
    n_inner = mesh.shape['cpi']

    def local_fn(hidden, w_q, w_k, w_v, w_o):
        tok, d_model = hidden.shape
        rank = lax.axis_index('cpo') * n_inner + lax.axis_index('cpi')
        positions = (rank * tok + jnp.arange(tok)).astype(jnp.float32)
        inv_freq = ROPE_BASE ** (-jnp.arange(HD // 2, dtype=jnp.float32) * 2.0 / HD)
        angles = positions[:, None] * inv_freq
        cos_t = jnp.cos(angles)
        sin_t = jnp.sin(angles)
        cos_full = jnp.concatenate([cos_t, cos_t], axis=1)
        sin_full = jnp.concatenate([-sin_t, sin_t], axis=1)
        any_spec = pl.BlockSpec(memory_space=pl.ANY)
        bf = jnp.bfloat16
        dma = pltpu.SemaphoreType.DMA
        return pl.pallas_call(
            body,
            out_shape=jax.ShapeDtypeStruct((tok, d_model), bf),
            in_specs=[any_spec] * 7,
            out_specs=any_spec,
            scratch_shapes=[
                pltpu.VMEM((tok, d_model), bf),
                pltpu.VMEM((tok, HD), jnp.float32),
                pltpu.VMEM((tok, HD), jnp.float32),
                pltpu.VMEM((d_model, 8, HD), bf),
                pltpu.VMEM((d_model, 8, HD), bf),
                pltpu.VMEM((GROUP, 2 * TOK, HD), bf),
                pltpu.VMEM((GROUP, 2 * TOK, HD), bf),
                pltpu.VMEM((GROUP + BACK, 2 * TOK, HD), bf),
                pltpu.VMEM((GROUP, 2 * TOK, HD), bf),
                pltpu.VMEM((BACK, TOK, 2 * TOK), jnp.float32),
                pltpu.VMEM((GROUP, TOK, 2 * HD), bf),
                pltpu.VMEM((GROUP, TOK, 2 * HD), bf),
                pltpu.VMEM((2, 4, HD, d_model), bf),
                pltpu.VMEM((tok, d_model), jnp.float32),
                pltpu.VMEM((tok, d_model), bf),
                dma((3,)), dma((2,)), dma((2,)), dma(()),
                dma((GROUP,)), dma((GROUP,)), dma((BACK,)), dma((BACK,)),
                dma((GROUP,)), dma((GROUP,)), dma((GROUP,)), dma((GROUP,)),
            ],
            compiler_params=pltpu.CompilerParams(collective_id=0, has_side_effects=True, vmem_limit_bytes=67043328),
        )(hidden, w_q, w_k, w_v, w_o, cos_full, sin_full)

    return jax.shard_map(local_fn, mesh=mesh,
                         in_specs=(P(('dp', 'cpo', 'cpi'), None), P(), P(), P(), P()),
                         out_specs=P(('dp', 'cpo', 'cpi'), None), check_vma=False)
```

profile of v0, /device:TPU:73, one launch (start us, length us, event | category | flops | bytes accessed | tf_op | source)
XLA Modules:
  0.0 130.6 jit_solution(12424062462792903501)
XLA Ops:
  0.0 0.5 fusion
  0.6 0.8 pad_maximum_fusion
  1.4 126.0 %shard_map.55 = bf16[256,4608]{1,0:T(8,128)(2,1)} custom-call(bf16[256,4608]{1,0:T(8,128)(2,1)} %x_hbm.1, bf16[4608,32,128]{2,1,0:T(8,128)(2,1)} %wq_hbm.1, bf16[4608,16,128]{2,1,0:T(8,128)(2,1)} %wk_hbm.1, bf16[4608,16,128]{2,1,0:T(8,128)(2,1)} %wv_hbm.1, bf16[32,128,4608]{2,1,0:T(8,128)(2,1)} %wo_hbm.1, f32[256,128]{1,0:T(8,128)} %get-tuple-element.8.cos_hbm, ...), custom_call_target="tpu_custom_call" | custom-call | tf_op jit(solution)/shard_map/pallas_call | solution.py:338
  127.4 3.2 %copy.7 = bf16[256,4608]{1,0:T(8,128)(2,1)} copy(bf16[256,4608]{1,0:T(8,128)(2,1)} %shard_map.55) | data formatting | bytes 4718592
  (2 shorter events, 0.0 us)
where the time goes:
time: 131 us
  Pallas kernels  126 us (96%)
  local copies, waits for them, and re-layouts  3.22 us (2%)
  other arithmetic  1.39 us (1%)
    pallas_call x1, Pallas kernels, local_fn(): pl.pallas_call(body, out_shape=jax.ShapeDtypeStruct((tok, d_model), bf),...  126 us
    unnamed x1, local copies, waits for them, and re-layouts  3.22 us

commit v1 on v0

v1 whole, which is shorter than its diff:
```python
import functools
import math

import jax
import jax.numpy as jnp
from jax import lax
from jax.experimental import pallas as pl
from jax.experimental.pallas import tpu as pltpu
from jax.sharding import PartitionSpec as P

ROPE_BASE = 10000.0
GROUP = 16
TOK = 256
HD = 128
BACK = 8
MESH = pl.DeviceIdType.MESH


def head_of(member):
    y = member // 4
    x = member % 4
    d = (x + 4 - y) % 4
    return 8 * (d % 2) + 4 * (d // 2) + y


def member_of(head):
    c = head // 8
    b = (head // 4) % 2
    y = head % 4
    return 4 * y + (y + c + 2 * b) % 4


def body(x_hbm, wq_hbm, wk_hbm, wv_hbm, wo_hbm, cos_hbm, sin_hbm, y_hbm,
         x_v, cos_v, sin_v, w0, w1, kv_out, q_out, kv_in, q_in, s_a, s_b, o_in, wo_buf, y_acc,
         in_sem, w_sem, wo_sem, y_sem, k_ss, k_rs, v_ss, v_rs, h_ss, h_rs, q_ss, q_rs, o_ss, o_rs):
    core = lax.axis_index('cpo')
    chip = lax.axis_index('cpi')
    z = chip // GROUP
    me = chip % GROUP
    base = z * GROUP
    my_y = me // 4
    my_class = (me % 4 + 4 - my_y) % 4
    my_head = head_of(me)
    d_model = x_v.shape[1]

    def eight(w_hbm, chunk):
        return w_hbm.at[:, pl.ds(pl.multiple_of(8 * chunk, 8), 8), :]

    def class_chunk(k):
        d = (my_class + k) % 4
        return 2 * (d % 2) + d // 2

    def w_load(w_hbm, chunk, slot):
        return pltpu.make_async_copy(eight(w_hbm, chunk), (w0, w1)[slot], w_sem.at[slot])

    x_copy = pltpu.make_async_copy(x_hbm, x_v, in_sem.at[0])
    cos_copy = pltpu.make_async_copy(cos_hbm, cos_v, in_sem.at[1])
    sin_copy = pltpu.make_async_copy(sin_hbm, sin_v, in_sem.at[2])
    first = my_class % 2
    x_copy.start()
    w_load(wk_hbm, first, 0).start()
    cos_copy.start()
    sin_copy.start()
    w_load(wv_hbm, first, 1).start()

    next_core = jnp.where(z == 3, 1 - core, core)
    next_chip = ((z + 1) % 4) * GROUP + me
    prev_core = jnp.where(z == 0, 1 - core, core)
    prev_chip = ((z + 3) % 4) * GROUP + me

    barrier = pltpu.get_barrier_semaphore()
    for step in range(1, GROUP):
        pl.semaphore_signal(barrier, inc=1, device_id={'cpi': base + (me + step) % GROUP}, device_id_type=MESH)
    pl.semaphore_signal(barrier, inc=1, device_id={'cpo': next_core, 'cpi': next_chip}, device_id_type=MESH)
    pl.semaphore_signal(barrier, inc=1, device_id={'cpo': prev_core, 'cpi': prev_chip}, device_id_type=MESH)
    pl.semaphore_wait(barrier, GROUP + 1)

    x_copy.wait()
    cos_copy.wait()
    sin_copy.wait()

    def project(w_ref):
        w = w_ref[...].reshape(d_model, 8 * HD)
        return jnp.dot(x_v[...], w, preferred_element_type=jnp.float32)

    def rope(u):
        return u * cos_v[...] + pltpu.roll(u, HD // 2, 1) * sin_v[...]

    k_rows = pl.ds(0, TOK)
    v_rows = pl.ds(TOK, TOK)

    def k_copy(head, dst_member, src):
        return pltpu.make_async_remote_copy(
            src_ref=kv_out.at[head, k_rows], dst_ref=kv_in.at[BACK + src, k_rows], send_sem=k_ss.at[head],
            recv_sem=k_rs.at[src], device_id={'cpi': base + dst_member}, device_id_type=MESH)

    def v_copy(head, dst_member, src):
        return pltpu.make_async_remote_copy(
            src_ref=kv_out.at[head, v_rows], dst_ref=kv_in.at[BACK + src, v_rows], send_sem=v_ss.at[head],
            recv_sem=v_rs.at[src], device_id={'cpi': base + dst_member}, device_id_type=MESH)

    def q_copy(head, dst_member, src):
        return pltpu.make_async_remote_copy(
            src_ref=q_out.at[head], dst_ref=q_in.at[src], send_sem=q_ss.at[head], recv_sem=q_rs.at[src],
            device_id={'cpi': base + dst_member}, device_id_type=MESH)

    def o_copy(block, head):
        return pltpu.make_async_remote_copy(
            src_ref=kv_out.at[block], dst_ref=o_in.at[head], send_sem=o_ss.at[block], recv_sem=o_rs.at[head],
            device_id={'cpi': base + block}, device_id_type=MESH)

    def halo(block):
        return pltpu.make_async_remote_copy(
            src_ref=kv_in.at[GROUP + block], dst_ref=kv_in.at[block], send_sem=h_ss.at[block], recv_sem=h_rs.at[block],
            device_id={'cpo': next_core, 'cpi': next_chip}, device_id_type=MESH)

    def send_class(copy, k):
        for step in range(4):
            y = (my_y + step) % 4
            head = 4 * class_chunk(k) + y

            def go(head=head):
                copy(head, member_of(head), me).start()

            if step == 0:
                pl.when(k > 0)(go)
            else:
                go()

    def kv_chunk(t, carry):
        c = (first + t) % 2
        w_load(wk_hbm, 0, 0).wait()
        k_all = project(w0)
        for i in range(8):
            kv_out[8 * c + i, 0:TOK, :] = rope(k_all[:, HD * i:HD * i + HD]).astype(jnp.bfloat16)

        @pl.when(t == 0)
        def _():
            w_load(wk_hbm, 1 - first, 0).start()

        @pl.when(t == 1)
        def _():
            w_load(wq_hbm, class_chunk(0), 0).start()

        send_class(k_copy, t)
        send_class(k_copy, t + 2)

        w_load(wv_hbm, 0, 1).wait()
        v_all = project(w1)
        for i in range(8):
            v_bf = v_all[:, HD * i:HD * i + HD].astype(jnp.bfloat16)
            kv_out[8 * c + i, TOK:TOK + HD, :] = v_bf[0:HD].T
            kv_out[8 * c + i, TOK + HD:TOK + 2 * HD, :] = v_bf[HD:TOK].T

        @pl.when(t == 0)
        def _():
            w_load(wv_hbm, 1 - first, 1).start()

        @pl.when(t == 1)
        def _():
            w_load(wq_hbm, class_chunk(1), 1).start()

        send_class(v_copy, t)
        send_class(v_copy, t + 2)
        return carry

    lax.fori_loop(0, 2, kv_chunk, 0)
    kv_in[BACK + me] = kv_out[my_head]

    def wait_kv(src):
        @pl.when(src != me)
        def _():
            k_copy(0, 0, src).wait_recv()
            v_copy(0, 0, src).wait_recv()

    def forward(parity):
        for i in range(4):
            y = 2 + i // 2
            src = 4 * y + (y + my_class + parity + 2 * (i % 2)) % 4
            wait_kv(src)
            halo(src - BACK).start()

    def q_store(slot_ref, k):
        q_all = project(slot_ref)
        j = class_chunk(k)
        for i in range(4):
            for g in range(2):
                lo = HD * (2 * i + g)
                q_out[4 * j + i, TOK * g:TOK * g + TOK, :] = rope(q_all[:, lo:lo + HD]).astype(jnp.bfloat16)

    def q_chunk(u, carry):
        for half in range(2):
            k = 2 * u + half
            w_load(wq_hbm, 0, half).wait()
            q_store((w0, w1)[half], k)

            @pl.when(u == 0)
            def _():
                w_load(wq_hbm, class_chunk(2 + half), half).start()

            send_class(q_copy, k)
        forward(u)
        return carry

    lax.fori_loop(0, 2, q_chunk, 0)

    n_wo = wo_buf.shape[0]

    def out_head(g):
        return 4 * class_chunk(g // 2) + 2 * (g % 2)

    def wo_copy(g):
        return pltpu.make_async_copy(wo_hbm.at[pl.ds(2 * out_head(g), 4)], wo_buf.at[g % n_wo], wo_sem.at[g % n_wo])

    for g in range(n_wo):
        wo_copy(g).start()

    q_in[me] = q_out[my_head]

    def kv_low(src, carry):
        wait_kv(src)
        return carry

    lax.fori_loop(0, BACK, kv_low, 0)

    def kv_drain(h, carry):
        @pl.when(h != my_head)
        def _():
            k_copy(h, 0, 0).wait_send()
            v_copy(h, 0, 0).wait_send()
        return carry

    lax.fori_loop(0, GROUP, kv_drain, 0)

    scale = HD ** -0.5 * math.log2(math.e)
    rows_k = lax.broadcasted_iota(jnp.int32, (TOK, 2 * TOK), 0)
    rows_q = lax.broadcasted_iota(jnp.int32, (TOK, 2 * TOK), 1) % TOK
    causal = rows_k <= rows_q
    is_first = (z == 0) & (core == 0)
    neg = jnp.float32(-jnp.inf)

    def biases(i):
        return [jnp.where(is_first & (i + j < BACK), neg, jnp.float32(0.0)) for j in range(BACK)]

    def scores(block, q):
        return lax.dot_general(kv_in[block, 0:TOK, :], q, (((1,), (1,)), ((), ())), preferred_element_type=jnp.float32)

    def v_of(block):
        return jnp.concatenate([kv_in[block, TOK:TOK + HD, :], kv_in[block, TOK + HD:TOK + 2 * HD, :]], axis=1)

    def score_tile(buf, i, q, j, bias, top):
        if j == 0:
            s = jnp.where(causal, scores(i + BACK, q), scores(i, q) + bias[0])
            buf[0] = s
            return jnp.max(s, axis=0, keepdims=True)
        s = scores(i + j, q)
        buf[j] = s
        return jnp.maximum(top, jnp.max(s, axis=0, keepdims=True) + bias[j])

    def pv_tile(buf, i, j, bias, top, total, acc):
        if j == 0:
            p = jnp.exp2(buf[0] * scale - top)
            zero = jnp.zeros_like(p)
            acc = jnp.dot(v_of(i + BACK), jnp.where(causal, p, zero).astype(jnp.bfloat16),
                          preferred_element_type=jnp.float32)
            acc += jnp.dot(v_of(i), jnp.where(causal, zero, p).astype(jnp.bfloat16),
                           preferred_element_type=jnp.float32)
            return jnp.sum(p, axis=0, keepdims=True), acc
        p = jnp.exp2(buf[j] * scale - (top - bias[j]))
        total = total + jnp.sum(p, axis=0, keepdims=True)
        return total, acc + jnp.dot(v_of(i + j), p.astype(jnp.bfloat16), preferred_element_type=jnp.float32)

    def stage(done, ahead):
        if ahead is not None:
            buf_n, i_n = ahead
            q = q_in[i_n]
            bias_n = biases(i_n)
        if done is not None:
            buf_d, i_d, top_d = done
            top_d = top_d * scale
            bias_d = biases(i_d)
        top_n = total = acc = None
        for j in range(BACK):
            if ahead is not None:
                top_n = score_tile(buf_n, i_n, q, j, bias_n, top_n)
            if done is not None:
                total, acc = pv_tile(buf_d, i_d, j, bias_d, top_d, total, acc)
        if done is not None:
            o = (acc / total).T
            kv_out[i_d] = o.astype(jnp.bfloat16)
        return top_n

    def out_step(g, carry):
        wo_copy(g).wait()
        head = out_head(g)
        for k in range(2):
            @pl.when(head + k != my_head)
            def _():
                o_copy(0, head + k).wait_recv()
        o = jnp.concatenate([o_in[head + k, TOK * g2:TOK * g2 + TOK] for k in range(2) for g2 in range(2)], axis=1)
        w = wo_buf[g % n_wo].reshape(4 * HD, d_model)
        part = jnp.dot(o, w, preferred_element_type=jnp.float32)

        @pl.when(g == 0)
        def _():
            y_acc[...] = part

        @pl.when(g > 0)
        def _():
            y_acc[...] += part

        @pl.when(g + n_wo < 8)
        def _():
            wo_copy(g + n_wo).start()
        return carry

    def attend_set(t, carry):
        blocks = []
        for n in range(4):
            y = (2 if n < 2 else 0) + (my_y + n) % 2
            blocks.append(4 * y + (y + my_class + 4 - t) % 4)
        bufs = (s_a, s_b, s_a, s_b)

        def wait_q(i):
            @pl.when(i != me)
            def _():
                q_copy(0, 0, i).wait_recv()

        def ship(i):
            @pl.when(i != me)
            def _():
                o_copy(i, my_head).start()

            @pl.when(i == me)
            def _():
                o_in[my_head] = kv_out[me]

        wait_q(blocks[0])
        top = stage(None, (bufs[0], blocks[0]))
        for n in range(4):
            if n == 1:
                @pl.when(t == 0)
                def _():
                    for b in range(BACK):
                        halo(b).wait_recv()
            if n < 3:
                wait_q(blocks[n + 1])
            top = stage((bufs[n], blocks[n], top), (bufs[n + 1], blocks[n + 1]) if n < 3 else None)
            ship(blocks[n])

        @pl.when(t > 0)
        def _():
            lax.fori_loop(2 * t - 2, 2 * t, out_step, 0)
        return carry

    lax.fori_loop(0, 4, attend_set, 0)
    lax.fori_loop(6, 8, out_step, 0)

    rows = TOK // 4
    y_copies = []
    for r in range(4):
        part = pl.ds(rows * r, rows)
        x_v[part, :] = y_acc[part, :].astype(jnp.bfloat16)
        y_copies.append(pltpu.make_async_copy(x_v.at[part], y_hbm.at[part], y_sem.at[r]))
    for y_copy in y_copies:
        y_copy.start()

    for b in range(BACK):
        halo(b).wait_send()

    def drain(h, carry):
        @pl.when(h != my_head)
        def _():
            q_copy(h, 0, 0).wait_send()

        @pl.when(h != me)
        def _():
            o_copy(h, 0).wait_send()
        return carry

    lax.fori_loop(0, GROUP, drain, 0)
    for y_copy in y_copies:
        y_copy.wait()


def solution(mesh):
    n_inner = mesh.shape['cpi']

    def local_fn(hidden, w_q, w_k, w_v, w_o):
        tok, d_model = hidden.shape
        rank = lax.axis_index('cpo') * n_inner + lax.axis_index('cpi')
        positions = (rank * tok + jnp.arange(tok)).astype(jnp.float32)
        inv_freq = ROPE_BASE ** (-jnp.arange(HD // 2, dtype=jnp.float32) * 2.0 / HD)
        angles = positions[:, None] * inv_freq
        cos_t = jnp.cos(angles)
        sin_t = jnp.sin(angles)
        cos_full = jnp.concatenate([cos_t, cos_t], axis=1)
        sin_full = jnp.concatenate([-sin_t, sin_t], axis=1)
        any_spec = pl.BlockSpec(memory_space=pl.ANY)
        bf = jnp.bfloat16
        dma = pltpu.SemaphoreType.DMA
        return pl.pallas_call(
            body,
            out_shape=jax.ShapeDtypeStruct((tok, d_model), bf),
            in_specs=[any_spec] * 7,
            out_specs=any_spec,
            scratch_shapes=[
                pltpu.VMEM((tok, d_model), bf),
                pltpu.VMEM((tok, HD), jnp.float32),
                pltpu.VMEM((tok, HD), jnp.float32),
                pltpu.VMEM((d_model, 8, HD), bf),
                pltpu.VMEM((d_model, 8, HD), bf),
                pltpu.VMEM((GROUP, 2 * TOK, HD), bf),
                pltpu.VMEM((GROUP, 2 * TOK, HD), bf),
                pltpu.VMEM((GROUP + BACK, 2 * TOK, HD), bf),
                pltpu.VMEM((GROUP, 2 * TOK, HD), bf),
                pltpu.VMEM((BACK, TOK, 2 * TOK), jnp.float32),
                pltpu.VMEM((BACK, TOK, 2 * TOK), jnp.float32),
                pltpu.VMEM((GROUP, 2 * TOK, HD), bf),
                pltpu.VMEM((2, 4, HD, d_model), bf),
                pltpu.VMEM((tok, d_model), jnp.float32),
                dma((3,)), dma((2,)), dma((2,)), dma((4,)),
                dma((GROUP,)), dma((GROUP,)), dma((GROUP,)), dma((GROUP,)), dma((BACK,)), dma((BACK,)),
                dma((GROUP,)), dma((GROUP,)), dma((GROUP,)), dma((GROUP,)),
            ],
            compiler_params=pltpu.CompilerParams(collective_id=0, has_side_effects=True, vmem_limit_bytes=67043328),
        )(hidden, w_q, w_k, w_v, w_o, cos_full, sin_full)

    return jax.shard_map(local_fn, mesh=mesh,
                         in_specs=(P(('dp', 'cpo', 'cpi'), None), P(), P(), P(), P()),
                         out_specs=P(('dp', 'cpo', 'cpi'), None), check_vma=False)
```

time: 131 us -> 115 us (0.88)
  the two profiles are of different devices: /device:TPU:73 before, /device:TPU:12 now
where the time goes in v1:
time: 115 us
  Pallas kernels  110 us (96%)
  local copies, waits for them, and re-layouts  3.22 us (3%)
  other arithmetic  1.39 us (1%)
    pallas_call x1, Pallas kernels, local_fn(): pl.pallas_call(body, out_shape=jax.ShapeDtypeStruct((tok, d_model), bf),...  110 us
    unnamed x1, local copies, waits for them, and re-layouts  3.22 us

profile of v1, /device:TPU:12, one launch (start us, length us, event | category | flops | bytes accessed | tf_op | source)
XLA Modules:
  0.0 114.6 jit_solution(3096742305441841234)
XLA Ops:
  0.0 0.5 fusion
  0.6 0.8 pad_maximum_fusion
  1.4 109.9 %shard_map.55 = bf16[256,4608]{1,0:T(8,128)(2,1)} custom-call(bf16[256,4608]{1,0:T(8,128)(2,1)} %x_hbm.1, bf16[4608,32,128]{2,1,0:T(8,128)(2,1)} %wq_hbm.1, bf16[4608,16,128]{2,1,0:T(8,128)(2,1)} %wk_hbm.1, bf16[4608,16,128]{2,1,0:T(8,128)(2,1)} %wv_hbm.1, bf16[32,128,4608]{2,1,0:T(8,128)(2,1)} %wo_hbm.1, f32[256,128]{1,0:T(8,128)} %get-tuple-element.8.cos_hbm, ...), custom_call_target="tpu_custom_call" | custom-call | tf_op jit(solution)/shard_map/pallas_call | solution.py:402
  111.3 3.2 %copy.7 = bf16[256,4608]{1,0:T(8,128)(2,1)} copy(bf16[256,4608]{1,0:T(8,128)(2,1)} %shard_map.55) | data formatting | bytes 4718592
  (2 shorter events, 0.0 us)

commit v2 on v1

--- a/solution.py
+++ b/solution.py
@@ -3,6 +3,7 @@
 
 import jax
 import jax.numpy as jnp
+import numpy as np
 from jax import lax
 from jax.experimental import pallas as pl
 from jax.experimental.pallas import tpu as pltpu
@@ -30,8 +31,8 @@
     return 4 * y + (y + c + 2 * b) % 4
 
 
-def body(x_hbm, wq_hbm, wk_hbm, wv_hbm, wo_hbm, cos_hbm, sin_hbm, y_hbm,
-         x_v, cos_v, sin_v, w0, w1, kv_out, q_out, kv_in, q_in, s_a, s_b, o_in, wo_buf, y_acc,
+def body(x_hbm, wq_hbm, wk_hbm, wv_hbm, wo_hbm, freq_hbm, y_hbm,
+         x_v, freq_v, cos_v, sin_v, w0, w1, kv_out, q_out, kv_in, q_in, s_a, s_b, o_in, wo_buf, y_acc,
          in_sem, w_sem, wo_sem, y_sem, k_ss, k_rs, v_ss, v_rs, h_ss, h_rs, q_ss, q_rs, o_ss, o_rs):
     core = lax.axis_index('cpo')
     chip = lax.axis_index('cpi')
@@ -43,25 +44,32 @@
     my_head = head_of(me)
     d_model = x_v.shape[1]
 
-    def eight(w_hbm, chunk):
-        return w_hbm.at[:, pl.ds(pl.multiple_of(8 * chunk, 8), 8), :]
-
     def class_chunk(k):
         d = (my_class + k) % 4
         return 2 * (d % 2) + d // 2
 
-    def w_load(w_hbm, chunk, slot):
-        return pltpu.make_async_copy(eight(w_hbm, chunk), (w0, w1)[slot], w_sem.at[slot])
-
-    x_copy = pltpu.make_async_copy(x_hbm, x_v, in_sem.at[0])
-    cos_copy = pltpu.make_async_copy(cos_hbm, cos_v, in_sem.at[1])
-    sin_copy = pltpu.make_async_copy(sin_hbm, sin_v, in_sem.at[2])
+    half_d = d_model // 2
+
+    def w_half(w_hbm, chunk, slot, part):
+        rows = pl.ds(half_d * part, half_d)
+        src = w_hbm.at[rows, pl.ds(pl.multiple_of(8 * chunk, 8), 8), :]
+        return pltpu.make_async_copy(src, (w0, w1)[slot].at[rows], w_sem.at[slot, part])
+
+    def w_start(w_hbm, chunk, slot):
+        for part in range(2):
+            w_half(w_hbm, chunk, slot, part).start()
+
+    def x_half(part):
+        cols = pl.ds(half_d * part, half_d)
+        return pltpu.make_async_copy(x_hbm.at[:, cols], x_v.at[:, cols], in_sem.at[part])
+
+    freq_copy = pltpu.make_async_copy(freq_hbm, freq_v, in_sem.at[2])
     first = my_class % 2
-    x_copy.start()
-    w_load(wk_hbm, first, 0).start()
-    cos_copy.start()
-    sin_copy.start()
-    w_load(wv_hbm, first, 1).start()
+    freq_copy.start()
+    for part in range(2):
+        x_half(part).start()
+        w_half(wk_hbm, first, 0, part).start()
+    w_start(wv_hbm, first, 1)
 
     next_core = jnp.where(z == 3, 1 - core, core)
     next_chip = ((z + 1) % 4) * GROUP + me
@@ -73,15 +81,29 @@
         pl.semaphore_signal(barrier, inc=1, device_id={'cpi': base + (me + step) % GROUP}, device_id_type=MESH)
     pl.semaphore_signal(barrier, inc=1, device_id={'cpo': next_core, 'cpi': next_chip}, device_id_type=MESH)
     pl.semaphore_signal(barrier, inc=1, device_id={'cpo': prev_core, 'cpi': prev_chip}, device_id_type=MESH)
+
+    freq_copy.wait()
+    pos = (core * (4 * GROUP) + chip) * TOK + lax.broadcasted_iota(jnp.int32, (TOK, HD), 0)
+    angle = pos.astype(jnp.float32) * freq_v[...]
+    low = lax.broadcasted_iota(jnp.int32, (TOK, HD), 1) < HD // 2
+    cos_v[...] = jnp.cos(angle)
+    sin_t = jnp.sin(angle)
+    sin_v[...] = jnp.where(low, -sin_t, sin_t)
+
     pl.semaphore_wait(barrier, GROUP + 1)
-
-    x_copy.wait()
-    cos_copy.wait()
-    sin_copy.wait()
-
-    def project(w_ref):
-        w = w_ref[...].reshape(d_model, 8 * HD)
-        return jnp.dot(x_v[...], w, preferred_element_type=jnp.float32)
+    x_half(0).wait()
+    x_half(1).wait()
+
+    def project(slot):
+        w_ref = (w0, w1)[slot]
+        cols = slice(8 * HD * slot, 8 * HD * slot + 8 * HD)
+        for part in range(2):
+            w_half(wk_hbm, 0, slot, part).wait()
+            w = w_ref[half_d * part:half_d * part + half_d].reshape(half_d, 8 * HD)
+            term = jnp.dot(x_v[:, half_d * part:half_d * part + half_d], w, preferred_element_type=jnp.float32)
+            if part == 0:
+                y_acc[:, cols] = term
+        return y_acc[:, cols] + term
 
     def rope(u):
         return u * cos_v[...] + pltpu.roll(u, HD // 2, 1) * sin_v[...]
@@ -129,24 +151,22 @@
 
     def kv_chunk(t, carry):
         c = (first + t) % 2
-        w_load(wk_hbm, 0, 0).wait()
-        k_all = project(w0)
+        k_all = project(0)
         for i in range(8):
             kv_out[8 * c + i, 0:TOK, :] = rope(k_all[:, HD * i:HD * i + HD]).astype(jnp.bfloat16)
 
         @pl.when(t == 0)
         def _():
-            w_load(wk_hbm, 1 - first, 0).start()
+            w_start(wk_hbm, 1 - first, 0)
 
         @pl.when(t == 1)
         def _():
-            w_load(wq_hbm, class_chunk(0), 0).start()
+            w_start(wq_hbm, class_chunk(0), 0)
 
         send_class(k_copy, t)
         send_class(k_copy, t + 2)
 
-        w_load(wv_hbm, 0, 1).wait()
-        v_all = project(w1)
+        v_all = project(1)
         for i in range(8):
             v_bf = v_all[:, HD * i:HD * i + HD].astype(jnp.bfloat16)
             kv_out[8 * c + i, TOK:TOK + HD, :] = v_bf[0:HD].T
@@ -154,11 +174,11 @@
 
         @pl.when(t == 0)
         def _():
-            w_load(wv_hbm, 1 - first, 1).start()
+            w_start(wv_hbm, 1 - first, 1)
 
         @pl.when(t == 1)
         def _():
-            w_load(wq_hbm, class_chunk(1), 1).start()
+            w_start(wq_hbm, class_chunk(1), 1)
 
         send_class(v_copy, t)
         send_class(v_copy, t + 2)
@@ -180,8 +200,8 @@
             wait_kv(src)
             halo(src - BACK).start()
 
-    def q_store(slot_ref, k):
-        q_all = project(slot_ref)
+    def q_store(slot, k):
+        q_all = project(slot)
         j = class_chunk(k)
         for i in range(4):
             for g in range(2):
@@ -191,19 +211,22 @@
     def q_chunk(u, carry):
         for half in range(2):
             k = 2 * u + half
-            w_load(wq_hbm, 0, half).wait()
-            q_store((w0, w1)[half], k)
+            q_store(half, k)
 
             @pl.when(u == 0)
             def _():
-                w_load(wq_hbm, class_chunk(2 + half), half).start()
+                w_start(wq_hbm, class_chunk(2 + half), half)
 
             send_class(q_copy, k)
-        forward(u)
+
+            @pl.when(u == half)
+            def _():
+                forward(half)
         return carry
 
     lax.fori_loop(0, 2, q_chunk, 0)
 
+    y_acc[...] = jnp.zeros_like(y_acc)
     n_wo = wo_buf.shape[0]
 
     def out_head(g):
@@ -290,29 +313,46 @@
             kv_out[i_d] = o.astype(jnp.bfloat16)
         return top_n
 
-    def out_step(g, carry):
+    n_cols = d_model // 4
+
+    def out_rows(head):
+        return jnp.concatenate([o_in[head + k, TOK * g2:TOK * g2 + TOK] for k in range(2) for g2 in range(2)], axis=1)
+
+    def out_ready(g):
         wo_copy(g).wait()
         head = out_head(g)
         for k in range(2):
             @pl.when(head + k != my_head)
             def _():
                 o_copy(0, head + k).wait_recv()
-        o = jnp.concatenate([o_in[head + k, TOK * g2:TOK * g2 + TOK] for k in range(2) for g2 in range(2)], axis=1)
+        return head
+
+    def out_step(g, carry):
+        head = out_ready(g)
+        o = out_rows(head)
         w = wo_buf[g % n_wo].reshape(4 * HD, d_model)
-        part = jnp.dot(o, w, preferred_element_type=jnp.float32)
-
-        @pl.when(g == 0)
-        def _():
-            y_acc[...] = part
-
-        @pl.when(g > 0)
-        def _():
-            y_acc[...] += part
+        for n in range(4):
+            cols = slice(n_cols * n, n_cols * n + n_cols)
+            y_acc[:, cols] += jnp.dot(o, w[:, cols], preferred_element_type=jnp.float32)
 
         @pl.when(g + n_wo < 8)
         def _():
             wo_copy(g + n_wo).start()
         return carry
+
+    def out_last():
+        head = out_ready(7)
+        o = out_rows(head)
+        w = wo_buf[7 % n_wo].reshape(4 * HD, d_model)
+        copies = []
+        for n in range(4):
+            cols = slice(n_cols * n, n_cols * n + n_cols)
+            y = y_acc[:, cols] + jnp.dot(o, w[:, cols], preferred_element_type=jnp.float32)
+            x_v[:, cols] = y.astype(jnp.bfloat16)
+            part = pl.ds(n_cols * n, n_cols)
+            copies.append(pltpu.make_async_copy(x_v.at[:, part], y_hbm.at[:, part], y_sem.at[n]))
+            copies[-1].start()
+        return copies
 
     def attend_set(t, carry):
         blocks = []
@@ -355,15 +395,12 @@
 
     lax.fori_loop(0, 4, attend_set, 0)
     lax.fori_loop(6, 8, out_step, 0)
-
-    rows = TOK // 4
     y_copies = []
     for r in range(4):
-        part = pl.ds(rows * r, rows)
+        part = pl.ds(TOK // 4 * r, TOK // 4)
         x_v[part, :] = y_acc[part, :].astype(jnp.bfloat16)
         y_copies.append(pltpu.make_async_copy(x_v.at[part], y_hbm.at[part], y_sem.at[r]))
-    for y_copy in y_copies:
-        y_copy.start()
+        y_copies[-1].start()
 
     for b in range(BACK):
         halo(b).wait_send()
@@ -388,24 +425,19 @@
 
     def local_fn(hidden, w_q, w_k, w_v, w_o):
         tok, d_model = hidden.shape
-        rank = lax.axis_index('cpo') * n_inner + lax.axis_index('cpi')
-        positions = (rank * tok + jnp.arange(tok)).astype(jnp.float32)
-        inv_freq = ROPE_BASE ** (-jnp.arange(HD // 2, dtype=jnp.float32) * 2.0 / HD)
-        angles = positions[:, None] * inv_freq
-        cos_t = jnp.cos(angles)
-        sin_t = jnp.sin(angles)
-        cos_full = jnp.concatenate([cos_t, cos_t], axis=1)
-        sin_full = jnp.concatenate([-sin_t, sin_t], axis=1)
+        inv_freq = ROPE_BASE ** (-np.arange(HD // 2) * 2.0 / HD)
+        freq = jnp.asarray(np.tile(np.concatenate([inv_freq, inv_freq])[None, :], (tok, 1)), jnp.float32)
         any_spec = pl.BlockSpec(memory_space=pl.ANY)
         bf = jnp.bfloat16
         dma = pltpu.SemaphoreType.DMA
         return pl.pallas_call(
             body,
             out_shape=jax.ShapeDtypeStruct((tok, d_model), bf),
-            in_specs=[any_spec] * 7,
+            in_specs=[any_spec] * 6,
             out_specs=any_spec,
             scratch_shapes=[
                 pltpu.VMEM((tok, d_model), bf),
+                pltpu.VMEM((tok, HD), jnp.float32),
                 pltpu.VMEM((tok, HD), jnp.float32),
                 pltpu.VMEM((tok, HD), jnp.float32),
                 pltpu.VMEM((d_model, 8, HD), bf),
@@ -419,12 +451,12 @@
                 pltpu.VMEM((GROUP, 2 * TOK, HD), bf),
                 pltpu.VMEM((2, 4, HD, d_model), bf),
                 pltpu.VMEM((tok, d_model), jnp.float32),
-                dma((3,)), dma((2,)), dma((2,)), dma((4,)),
+                dma((3,)), dma((2, 2)), dma((2,)), dma((4,)),
                 dma((GROUP,)), dma((GROUP,)), dma((GROUP,)), dma((GROUP,)), dma((BACK,)), dma((BACK,)),
                 dma((GROUP,)), dma((GROUP,)), dma((GROUP,)), dma((GROUP,)),
             ],
             compiler_params=pltpu.CompilerParams(collective_id=0, has_side_effects=True, vmem_limit_bytes=67043328),
-        )(hidden, w_q, w_k, w_v, w_o, cos_full, sin_full)
+        )(hidden, w_q, w_k, w_v, w_o, freq)
 
     return jax.shard_map(local_fn, mesh=mesh,
                          in_specs=(P(('dp', 'cpo', 'cpi'), None), P(), P(), P(), P()),

time: 115 us -> 106 us (0.922)
  the two profiles are of different devices: /device:TPU:12 before, /device:TPU:97 now
where the time goes in v2:
time: 106 us
  Pallas kernels  103 us (97%)
  local copies, waits for them, and re-layouts  3.22 us (3%)
    pallas_call x1, Pallas kernels, local_fn(): pl.pallas_call(body, out_shape=jax.ShapeDtypeStruct((tok, d_model), bf),...  103 us
    unnamed x1, local copies, waits for them, and re-layouts  3.22 us

profile of v2, /device:TPU:97, one launch (start us, length us, event | category | flops | bytes accessed | tf_op | source)
XLA Modules:
  0.0 105.9 jit_solution(15656612206199156799)
XLA Ops:
  0.0 102.7 %shard_map.64 = bf16[256,4608]{1,0:T(8,128)(2,1)} custom-call(bf16[256,4608]{1,0:T(8,128)(2,1)} %x_hbm.1, bf16[4608,32,128]{2,1,0:T(8,128)(2,1)} %wq_hbm.1, bf16[4608,16,128]{2,1,0:T(8,128)(2,1)} %wk_hbm.1, bf16[4608,16,128]{2,1,0:T(8,128)(2,1)} %wv_hbm.1, bf16[32,128,4608]{2,1,0:T(8,128)(2,1)} %wo_hbm.1, f32[256,128]{1,0:T(8,128)} %constant.2.clone.freq_hbm), custom_call_target="tpu_custom_call" | custom-call | tf_op jit(solution)/shard_map/pallas_call | solution.py:433
  102.7 3.2 %copy.8 = bf16[256,4608]{1,0:T(8,128)(2,1)} copy(bf16[256,4608]{1,0:T(8,128)(2,1)} %shard_map.64) | data formatting | bytes 4718592

commit v3 on v2

--- a/solution.py
+++ b/solution.py
@@ -390,11 +390,11 @@
 
         @pl.when(t > 0)
         def _():
-            lax.fori_loop(2 * t - 2, 2 * t, out_step, 0)
+            lax.fori_loop(t - 1, t, out_step, 0)
         return carry
 
     lax.fori_loop(0, 4, attend_set, 0)
-    lax.fori_loop(6, 8, out_step, 0)
+    lax.fori_loop(3, 8, out_step, 0)
     y_copies = []
     for r in range(4):
         part = pl.ds(TOK // 4 * r, TOK // 4)

time: 106 us -> 107 us (level)
  no operation moved by 1% of the time
where the time goes in v3:
time: 107 us
  Pallas kernels  103 us (96%)
  local copies, waits for them, and re-layouts  3.22 us (3%)
    pallas_call x1, Pallas kernels, local_fn(): pl.pallas_call(body, out_shape=jax.ShapeDtypeStruct((tok, d_model), bf),...  103 us
    unnamed x1, local copies, waits for them, and re-layouts  3.22 us

profile of v3, /device:TPU:97, one launch (start us, length us, event | category | flops | bytes accessed | tf_op | source)
XLA Modules:
  0.0 106.6 jit_solution(10088606999324920946)
XLA Ops:
  0.0 103.4 %shard_map.64 = bf16[256,4608]{1,0:T(8,128)(2,1)} custom-call(bf16[256,4608]{1,0:T(8,128)(2,1)} %x_hbm.1, bf16[4608,32,128]{2,1,0:T(8,128)(2,1)} %wq_hbm.1, bf16[4608,16,128]{2,1,0:T(8,128)(2,1)} %wk_hbm.1, bf16[4608,16,128]{2,1,0:T(8,128)(2,1)} %wv_hbm.1, bf16[32,128,4608]{2,1,0:T(8,128)(2,1)} %wo_hbm.1, f32[256,128]{1,0:T(8,128)} %constant.2.clone.freq_hbm), custom_call_target="tpu_custom_call" | custom-call | tf_op jit(solution)/shard_map/pallas_call | solution.py:433
  103.4 3.2 %copy.8 = bf16[256,4608]{1,0:T(8,128)(2,1)} copy(bf16[256,4608]{1,0:T(8,128)(2,1)} %shard_map.64) | data formatting | bytes 4718592
